TPU v7x, 32 devices: a whole 2x2x4 slice. The times are simulated.
32 devices in a mesh: tok: 16 (over z, y, x), head: 2 (over core).
Axes of the slice: x: 2, y: 2, z: 4, core: 2. Of those that a mesh axis runs over, the one named last changes fastest.
Arguments:
- text_queries: bfloat16 [256, 8192], P('tok', 'head'), may hold values from -6 to 6
- text_grads: bfloat16 [256, 8192], P('tok', 'head'), may hold values from -6 to 6
- vision_keys: bfloat16 [8192, 1024], P('tok', 'head'), may hold values from -6 to 6
- video_value_rows: bfloat16 [8192, 1024], P('tok', 'head'), may hold values from -6 to 6
- vision: bfloat16 [8192, 4096], P('tok'), may hold values from -6 to 6
- lengths: int32 [8], replicated, may hold values from 16 to 48, as said below
- frame_range: int32 [8, 2], replicated, may hold values from 0 to 64, as said below
Outputs:
- query_grad: bfloat16 [256, 8192], P(None, 'head')
- key_weight_grad: float32 [4096, 1024], P('tok', 'head')
- value_weight_grad: float32 [4096, 1024], P('tok', 'head')
Inputs may be any that keep to these rules, and one draw needn't show every extreme that they name: Each segment holds at least one row; the lengths sum to 256. `frame_range`: each segment's range covers 64 // 4 frames or more, first entry below the second.
All inputs are finite; a program needn't handle non-finite values.
Results may differ from a plain program's by a relative error of at most 0.0073.
Values may be sent and summed in bfloat16 or wider, within the bound.
A program may use at most 128 MiB of HBM per device.

v0:
```python
import jax
import jax.numpy as jnp
from jax import lax
from jax.sharding import PartitionSpec as P

HEAD_WIDTH = 128
FRAME_DEV = 4


NEG_FILL = -1e30


def shards(text_queries, text_grads, vision_keys, video_value_rows, vision, lengths, frame_range):
    feature_block = lax.all_to_all(vision, "tok", split_axis=1, concat_axis=0, tiled=True)
    text_q, text_g = (
        lax.all_gather(text_queries, "tok", axis=0, tiled=True),
        lax.all_gather(text_grads, "tok", axis=0, tiled=True),
    )
    text_len = text_q.shape[0]
    kv_rows = vision_keys.shape[0]
    kv_local = vision_keys.shape[1] // HEAD_WIDTH
    group_width = text_q.shape[1] // vision_keys.shape[1]
    score_scale = HEAD_WIDTH ** (-0.5)
    row_ids = jnp.arange(text_len, dtype=jnp.int32)
    segment_ends = jnp.cumsum(lengths)
    segment = jnp.sum((row_ids[:, None] >= segment_ends[None, :]).astype(jnp.int32), axis=1)
    segment_pick = (
        segment[:, None] == jnp.arange(lengths.shape[0], dtype=jnp.int32)[None, :]
    ).astype(jnp.int32)
    first_frame = jnp.sum(segment_pick * frame_range[None, :, 0], axis=1)
    end_frame = jnp.sum(segment_pick * frame_range[None, :, 1], axis=1)
    key_ids = lax.axis_index("tok") * kv_rows + jnp.arange(kv_rows, dtype=jnp.int32)
    frames = key_ids // (kv_rows // FRAME_DEV)
    allowed = (frames[None, :] >= first_frame[:, None]) & (frames[None, :] < end_frame[:, None])
    query_member = text_q.reshape(text_len, kv_local, group_width, HEAD_WIDTH).transpose(2, 0, 1, 3)
    grad_member = text_g.reshape(text_len, kv_local, group_width, HEAD_WIDTH).transpose(2, 0, 1, 3)
    key_three = vision_keys.reshape(kv_rows, kv_local, HEAD_WIDTH)
    value_three = video_value_rows.reshape(kv_rows, kv_local, HEAD_WIDTH)

    def scores_of(query_one, grad_one):
        scores = (
            jnp.einsum("ihd,jhd->hij", query_one, key_three, preferred_element_type=jnp.float32)
            * score_scale
        )
        dprobs = jnp.einsum(
            "ihd,jhd->hij", grad_one, value_three, preferred_element_type=jnp.float32
        )
        return (scores, dprobs)

    def local_stats(carry, member):
        scores, dprobs = scores_of(member[0], member[1])
        local_max = jnp.max(jnp.where(allowed, scores, NEG_FILL), axis=2)
        local_exp = jnp.where(allowed, jnp.exp(scores - local_max[..., None]), 0.0)
        return (carry, (local_max, jnp.sum(local_exp, axis=2), jnp.sum(local_exp * dprobs, axis=2)))

    unused, (local_max, local_sum, local_dot) = lax.scan(
        local_stats, jnp.zeros((), jnp.float32), (query_member, grad_member)
    )
    row_max = lax.pmax(local_max, "tok")
    rescale = jnp.exp(local_max - row_max)
    row_sum, row_dot = lax.psum((local_sum * rescale, local_dot * rescale), "tok")

    def member_grads(running, member):
        query_one, grad_one, max_one, sum_one, dot_one = member
        scores, dprobs = scores_of(query_one, grad_one)
        exp_terms = jnp.where(allowed, jnp.exp(scores - max_one[..., None]), 0.0)
        attn_probs = exp_terms / sum_one[..., None]
        row_delta = dot_one / sum_one
        dscore = (attn_probs * (dprobs - row_delta[..., None])).astype(jnp.bfloat16)
        value_sum = running[1] + jnp.einsum(
            "hij,ihd->jhd",
            attn_probs.astype(jnp.bfloat16),
            grad_one,
            preferred_element_type=jnp.float32,
        )
        key_sum = running[0] + jnp.einsum(
            "hij,ihd->jhd", dscore, query_one, preferred_element_type=jnp.float32
        )
        query_part = score_scale * jnp.einsum(
            "hij,jhd->ihd", dscore, key_three, preferred_element_type=jnp.float32
        )
        return ((key_sum, value_sum), query_part)

    zero_acc = jnp.zeros((kv_rows, kv_local, HEAD_WIDTH), jnp.float32)
    (key_sum, value_sum), query_parts = lax.scan(
        member_grads, (zero_acc, zero_acc), (query_member, grad_member, row_max, row_sum, row_dot)
    )
    key_grad = (score_scale * key_sum).astype(jnp.bfloat16)
    value_grad = value_sum.astype(jnp.bfloat16)
    query_part = query_parts.transpose(1, 2, 0, 3).reshape(text_len, -1)
    query_grad = lax.psum(query_part, "tok").astype(jnp.bfloat16)
    kv_data = jnp.concatenate(
        (key_grad.reshape(kv_rows, -1), value_grad.reshape(kv_rows, -1)), axis=1
    )
    half_width = kv_data.shape[1] // 2
    weight_grads = jnp.einsum(
        "tf,tc->fc",
        feature_block,
        lax.all_gather(kv_data, "tok", axis=0, tiled=True),
        preferred_element_type=jnp.float32,
    )
    return (query_grad, weight_grads[:, :half_width], weight_grads[:, half_width:])


def solution(mesh):
    return jax.shard_map(
        shards,
        mesh=mesh,
        in_specs=(
            P("tok", "head"),
            P("tok", "head"),
            P("tok", "head"),
            P("tok", "head"),
            P("tok", None),
            P(),
            P(),
        ),
        out_specs=(P(None, "head"), P("tok", "head"), P("tok", "head")),
        check_vma=False,
    )
```

profile of v0, /device:TPU:8, one launch (start us, length us, event | category | flops | bytes accessed | tf_op | source)
XLA Modules:
  0.0 831.9 jit_solution(17630682502274391698)
XLA Ops:
  11.8 60.5 %all-gather.4.cloned.1.call-done = bf16[256,4096]{1,0:T(8,128)(2,1)} async-done(((bf16[16,4096]{1,0:T(8,128)(2,1)}), bf16[256,4096]{1,0:T(8,128)(2,1)}) %all-gather.4.cloned.1.call-update) | async-done | bytes 2097168 | tf_op jit(solution)/shard_map/all_gather | solution.py:16
  72.3 4.1 copy.72
  76.4 3.0 copy.80
  79.4 54.9 %all-gather.6.cloned.1.call-done = bf16[256,4096]{1,0:T(8,128)(2,1)} async-done(((bf16[16,4096]{1,0:T(8,128)(2,1)}), bf16[256,4096]{1,0:T(8,128)(2,1)}) %all-gather.6.cloned.1.call-update) | async-done | bytes 2097168 | tf_op jit(solution)/shard_map/all_gather | solution.py:17
  134.3 4.1 copy.74
  138.3 4.0 copy.78
  142.3 26.8 %while.30 = (s32[]{:T(128)}, f32[8,4,256]{2,1,0:T(4,128)S(1)}, f32[8,4,256]{2,1,0:T(4,128)S(1)}, f32[8,4,256]{2,1,0:T(4,128)S(1)}, bf16[8,256,4,128]{3,1,2,0:T(8...) while((s32[]{:T(128)}, f32[8,4,256]{2,1,0:T(4,128)S(1)}, ...), condition=%wide.region_8.9_spmd.clone, body=%wide.region_4.8_spmd.clone.sunk | while | flops 275117056 | bytes 8437901 | solution.py:56
  143.8 1.8 multiply_reduce_fusion.2
  147.2 1.8 multiply_reduce_fusion.2
  150.5 1.8 multiply_reduce_fusion.2
  153.9 1.8 multiply_reduce_fusion.2
  157.2 1.8 multiply_reduce_fusion.2
  160.6 1.8 multiply_reduce_fusion.2
  163.9 1.8 multiply_reduce_fusion.2
  167.3 1.8 multiply_reduce_fusion.2
  169.1 68.3 %pmax.7 = f32[8,4,256]{2,1,0:T(4,128)S(1)} all-reduce(f32[8,4,256]{2,1,0:T(4,128)S(1)} %get-tuple-element.116), channel_id=1, replica_groups=mesh['tok'=16,'head'=2] {'tok'}, use_global_device_ids=true, to_apply=%region_9.10 | all-reduce | flops 8192 | bytes 65536 | tf_op jit(solution)/shard_map/pmax | solution.py:59
  238.2 105.5 %all-reduce.4.cloned.1.call-done = (f32[8,4,256]{2,1,0:T(4,128)}, f32[8,4,256]{2,1,0:T(4,128)}) async-done(((f32[8,4,256]{2,1,0:T(4,128)}, f32[8,4,256]{2,1,0:T(4,128)}), (f32[8,4,256]{2,1,0:T(4,128)}, f32[8,4,256]{2,1,0:T(4,128)})) %all-reduce.4.cloned.1.call-update) | async-done | bytes 65552 | tf_op jit(solution)/shard_map/psum | solution.py:61
  343.7 69.8 %while.31 = (s32[]{:T(128)}, f32[512,4,128]{0,2,1:T(8,128)S(1)}, f32[512,4,128]{0,2,1:T(8,128)S(1)}, f32[8,256,4,128]{3,1,2,0:T(8,128)}, bf16[8,256,4,128]{3,1,2...) while((s32[]{:T(128)}, f32[512,4,128]{0,2,1:T(8,128)S(1)}, ...), condition=%wide.region_13.14_spmd.clone, body=%wide.region_12.13_spmd.clone.sunk | while | flops 676856832 | bytes 17084612 | solution.py:85
  345.3 1.7 select_divide_fusion.2
  347.0 1.4 multiply_convert_fusion.3
  348.4 1.4 fusion.76
  354.1 1.7 select_divide_fusion.2
  355.7 1.4 multiply_convert_fusion.3
  357.2 1.4 fusion.76
  362.8 1.7 select_divide_fusion.2
  365.9 1.4 fusion.76
  371.5 1.7 select_divide_fusion.2
  374.6 1.4 fusion.76
  380.2 1.7 select_divide_fusion.2
  381.9 1.4 multiply_convert_fusion.3
  383.3 1.4 fusion.76
  388.9 1.7 select_divide_fusion.2
  390.6 1.4 multiply_convert_fusion.3
  392.1 1.4 fusion.76
  397.7 1.7 select_divide_fusion.2
  399.4 1.4 multiply_convert_fusion.3
  400.8 1.4 fusion.76
  406.4 1.7 select_divide_fusion.2
  408.1 1.4 multiply_convert_fusion.3
  409.5 1.4 fusion.76
  414.9 6.5 copy.85
  421.4 5.9 all-to-all-start
  427.2 4.6 copy.84
  431.9 5.8 copy.93
  437.6 356.3 %all-reduce.5 = bf16[256,4096]{1,0:T(8,128)(2,1)} all-reduce(f32[256,4096]{1,0:T(8,128)} %bitcast.132), channel_id=1, replica_groups=mesh['tok'=16,'head'=2] {'tok'}, use_global_device_ids=true, to_apply=%region_14.15 | all-reduce | flops 1048576 | bytes 6291456 | tf_op jit(solution)/shard_map/psum | solution.py:91
  793.9 6.4 copy.86
  800.3 13.6 %all-gather.8.cloned.1.call-done = bf16[8192,1024]{0,1:T(8,128)(2,1)} async-done(((bf16[512,1024]{0,1:T(8,128)(2,1)}), bf16[8192,1024]{0,1:T(8,128)(2,1)}) %all-gather.8.cloned.1.call-update) | async-done | bytes 16777232 | tf_op jit(solution)/shard_map/all_gather | solution.py:99
  814.0 9.3 %convolution_bitcast_fusion.2 = f32[256,1024]{0,1:T(8,128)S(1)} fusion(bf16[8192,1024]{0,1:T(8,128)(2,1)} %all-gather.8.cloned.1.call-done, bf16[8192,256]{1,0:T(8,128)(2,1)} %bitcast.136), kind=kOutput, calls=%fused_computation.44 | convolution fusion | flops 4294967296 | bytes 22020096 | tf_op jit(solution)/shard_map/tf,tc->fc/dot_general | solution.py:96
  (119 shorter events, 57.2 us)
Async XLA Ops:
  7.2 4.0 copy-start.1
  7.2 65.1 %all-gather.4.cloned.1.call-start = ((), (), s32[]{:S(2)}) async-start(), calls=%async_computation.1 | async-start | bytes 2228224 | tf_op jit(solution)/shard_map/all_gather | solution.py:16
  7.9 126.4 %all-gather.6.cloned.1.call-start = ((), (), s32[]{:S(2)}) async-start(), calls=%async_computation.2 | async-start | bytes 2228224 | tf_op jit(solution)/shard_map/all_gather | solution.py:17
  8.7 335.1 %all-reduce.4.cloned.1.call-start = ((), (), s32[]{:S(2)}) async-start(), calls=%async_computation.4 | async-start | bytes 131072 | tf_op jit(solution)/shard_map/psum | solution.py:61
  9.6 2.2 copy-start.2
  169.1 69.1 %copy-start = (bf16[8,256,4,128]{3,1,2,0:T(8,128)(2,1)}, bf16[8,256,4,128]{3,1,2,0:T(8,128)(2,1)S(1)}, u32[]{:S(2)}) copy-start(bf16[8,256,4,128]{3,1,2,0:T(8,128)(2,1)S(1)} %get-tuple-element.641) | copy-start | bytes 6291460
  238.1 575.8 %all-gather.8.cloned.1.call-start = ((), (), s32[]{:S(2)}) async-start(), calls=%async_computation.3 | async-start | bytes 17825792 | tf_op jit(solution)/shard_map/all_gather | solution.py:99
  421.4 372.5 %all-to-all-start = ((bf16[512,16,256]{0,2,1:T(8,128)(2,1)}), bf16[512,16,256]{0,2,1:T(8,128)(2,1)}, u32[]{:S(2)}, u32[]{:S(2)}) async-start(bf16[512,16,256]{0,2,1:T(8,128)(2,1)} %bitcast.130), calls=%async_computation | async-start | bytes 8388608 | tf_op jit(solution)/shard_map/all_to_all | solution.py:14
Sparse Core Ops, SparseCore 0:
  10.8 61.4 all-gather.3
  75.1 59.1 all-gather.5
  238.3 105.3 all-reduce.3
  415.0 398.8 all-gather.7
where the time goes:
time: 846 us; the launch traced here: 832 us
  blocking collectives  425 us (50%)
  waiting for transfers between devices  236 us (28%)
  matrix products  85.3 us (10%)
  local copies, waits for them, and re-layouts  48.1 us (6%)
  other arithmetic  17.4 us (2%)
  between operations  13.9 us (2%)
    psum x1, blocking collectives, shards(): query_grad = lax.psum(query_part, 'tok').astype(jnp.bfloat16)  356 us
    psum x1, waiting for transfers between devices, shards(): lax.psum((local_sum * rescale, local_dot * rescale), 'tok')  105 us
    pmax x1, blocking collectives, shards(): row_max = lax.pmax(local_max, 'tok')  68.3 us
    all_gather x1, waiting for transfers between devices, shards(): lax.all_gather(text_queries, 'tok', axis=0, tiled=True)  60.5 us
    all_gather x1, waiting for transfers between devices, shards(): lax.all_gather(text_grads, 'tok', axis=0, tiled=True)  54.9 us
    dot_general x16, matrix products, scores_of(): jnp.einsum('ihd,jhd->hij', grad_one, value_three, preferred_element_type=...  25.6 us
    unnamed x16, local copies, waits for them, and re-layouts  23.2 us
    dot_general x16, matrix products, scores_of(): jnp.einsum('ihd,jhd->hij', query_one, key_three, preferred_element_type=j...  18.1 us
  transfers between devices with their start and end apart: 5, of which 4 were waited for; matrix products, arithmetic and copies ran while one was open for 4% of the time, Pallas kernels for 0%

commit v1 on v0

v1 whole, which is shorter than its diff:
```python
import functools

import jax
import jax.numpy as jnp
from jax import lax
from jax.experimental import pallas as pl
from jax.experimental.pallas import tpu as pltpu
from jax.sharding import PartitionSpec as P

HEAD_WIDTH = 128
FRAME_DEV = 4
NEG_FILL = -1e30
NT = (((1,), (1,)), ((), ()))
TN = (((0,), (0,)), ((), ()))
F32 = jnp.float32
BF16 = jnp.bfloat16


def dot(a, b, dims=(((1,), (0,)), ((), ()))):
    return lax.dot_general(a, b, dims, preferred_element_type=F32)


def kernel(cfg, q_in, g_in, k_in, v_in, x_in, bounds, q_out, kw_out, vw_out,
           qb, gb, kb, vb, vis, ebuf, dpb, stat, stin, coef, kv, dqt, dqs, dqin, dqall, part, rsb,
           loc, qs, qr, gs, gr, ks, kr, vs, vr, xs, xr, ss, sr, kvs, kvr, ds, dr, as_, ar, ys, yr, rs, rr):
    T, G, NZ = cfg["T"], cfg["G"], cfg["NZ"]
    blk, rows, NK, NR, FR = cfg["blk"], cfg["rows"], cfg["NK"], cfg["NR"], cfg["FR"]
    W, NV, FB = cfg["W"], cfg["NV"], cfg["FB"]
    RB = cfg["RB"]
    scale = HEAD_WIDTH ** (-0.5)
    me = lax.axis_index("tok")
    z, j0 = me // G, me % G

    def remote(src, dst, s, r, peer):
        return pltpu.make_async_remote_copy(
            src_ref=src, dst_ref=dst, send_sem=s, recv_sem=r,
            device_id={"tok": peer}, device_id_type=pl.DeviceIdType.MESH)

    def m128(i, n):
        return pl.ds(pl.multiple_of(i * n, n), n)

    barrier = pltpu.get_barrier_semaphore()
    for d in range(1, T):
        pl.semaphore_signal(barrier, inc=1, device_id={"tok": lax.rem(me + d, T)}, device_id_type=pl.DeviceIdType.MESH)
    pl.semaphore_wait(barrier, T - 1)

    def tpeer(d):
        return lax.rem(me + d, T), lax.rem(me + T - d, T)

    def gpeer(d):
        a, b = lax.rem(j0 + d, G), lax.rem(j0 + G - d, G)
        return a, b, z * G + a, z * G + b

    def zpeer(d):
        a, b = lax.rem(z + d, NZ), lax.rem(z + NZ - d, NZ)
        return a, b, a * G + j0, b * G + j0

    sends = []

    def send(c):
        c.start()
        sends.append(c)

    def q_copy(t_to, t_from):
        return (remote(q_in.at[lax.rem(t_to, G)], qb.at[m128(t_from, blk)], qs.at[t_to], qr.at[t_from], t_to),
                remote(g_in.at[lax.rem(t_to, G)], gb.at[m128(t_from, blk)], gs.at[t_to], gr.at[t_from], t_to))

    def k_copy(j_to, j_from, peer):
        return (remote(k_in.at[:, m128(j_to, 128)], kb.at[m128(j_from, rows)], ks.at[j_to], kr.at[j_from], peer),
                remote(v_in.at[:, m128(j_to, 128)], vb.at[m128(j_from, rows)], vs.at[j_to], vr.at[j_from], peer))

    def x_copy(b, j_to, j_from, peer):
        return remote(x_in.at[:, m128(b * G + j_to, W)], vis.at[b, m128(j_from, rows)], xs.at[j_to, b], xr.at[j_from, b], peer)

    local = [
        pltpu.make_async_copy(q_in.at[j0], qb.at[m128(me, blk)], loc.at[0]),
        pltpu.make_async_copy(g_in.at[j0], gb.at[m128(me, blk)], loc.at[1]),
        pltpu.make_async_copy(k_in.at[:, m128(j0, 128)], kb.at[m128(j0, rows)], loc.at[2]),
        pltpu.make_async_copy(v_in.at[:, m128(j0, 128)], vb.at[m128(j0, rows)], loc.at[3]),
    ]
    local_x = [pltpu.make_async_copy(x_in.at[:, m128(b * G + j0, W)], vis.at[b, m128(j0, rows)], loc.at[4 + b]) for b in range(NV)]
    for c in local:
        c.start()
    for d in range(1, T):
        to, _ = tpeer(d)
        for c in q_copy(to, me):
            send(c)
    for d in range(1, G):
        a, _, peer, _ = gpeer(d)
        for c in k_copy(a, j0, peer):
            send(c)
    for c in local_x:
        c.start()
    for d in range(1, G):
        a, _, peer, _ = gpeer(d)
        for b in range(NV):
            send(x_copy(b, a, j0, peer))
    for c in local:
        c.wait()
    for d in range(1, G):
        _, b, _, _ = gpeer(d)
        for c in k_copy(j0, b, me):
            c.wait_recv()
    for d in range(1, T):
        _, frm = tpeer(d)
        for c in q_copy(me, frm):
            c.wait_recv()

    n_frames = NK // FR
    frame0 = z * n_frames
    stat[0:1, :] = jnp.full((1, NR), NEG_FILL, F32)
    stat[1:8, :] = jnp.zeros((7, NR), F32)

    @pl.loop(0, n_frames)
    def _(f):
        kc = kb[m128(f, FR), :]
        for r in range(0, NR, RB):
            cols = pl.ds(r, RB)
            ok = (bounds[0:1, cols] <= frame0 + f) & (frame0 + f < bounds[1:2, cols])
            s = jnp.where(ok, dot(kc, qb[cols, :], NT) * scale, NEG_FILL)
            ebuf[m128(f, FR), cols] = s
            stat[0:1, cols] = jnp.maximum(stat[0:1, cols], jnp.max(s, axis=0, keepdims=True))

    @pl.loop(0, n_frames)
    def _(f):
        vc = vb[m128(f, FR), :]
        for r in range(0, NR, RB):
            cols = pl.ds(r, RB)
            dp = dot(vc, gb[cols, :], NT)
            e = jnp.exp(ebuf[m128(f, FR), cols] - stat[0:1, cols])
            ebuf[m128(f, FR), cols] = e
            dpb[m128(f, FR), cols] = dp
            stat[1:2, cols] += jnp.sum(e, axis=0, keepdims=True)
            stat[2:3, cols] += jnp.sum(e * dp, axis=0, keepdims=True)

    def s_copy(z_to, z_from, peer):
        return remote(stat, stin.at[z_from], ss.at[z_to], sr.at[z_from], peer)

    for d in range(1, NZ):
        a, _, peer, _ = zpeer(d)
        send(s_copy(a, z, peer))
    stin[z] = stat[...]
    for d in range(1, NZ):
        _, b, _, _ = zpeer(d)
        s_copy(z, b, me).wait_recv()
    top = stat[0:1, :]
    for i in range(NZ):
        top = jnp.maximum(top, stin[i, 0:1, :])
    total = jnp.zeros((1, NR), F32)
    dotted = jnp.zeros((1, NR), F32)
    for i in range(NZ):
        w = jnp.exp(stin[i, 0:1, :] - top)
        total += w * stin[i, 1:2, :]
        dotted += w * stin[i, 2:3, :]
    coef[0:1, :] = jnp.exp(stat[0:1, :] - top) / total
    coef[1:2, :] = dotted / total
    dqt[...] = jnp.zeros_like(dqt)

    NC = cfg["NC"]
    CH = NK // NC

    def kv_copy(c, j_to, j_from, peer):
        here = kv.at[j_from, pl.ds(c * CH, CH)]
        return remote(here, here, kvs.at[j_to, c], kvr.at[j_from, c], peer)

    for c in range(NC):
        @pl.loop(c * (CH // FR), (c + 1) * (CH // FR))
        def _(f):
            kt = kb[m128(f, FR), :].astype(F32).T.astype(BF16)
            dk = jnp.zeros((FR, HEAD_WIDTH), F32)
            dv = jnp.zeros((FR, HEAD_WIDTH), F32)
            for r in range(0, NR, RB):
                cols = pl.ds(r, RB)
                p = ebuf[m128(f, FR), cols] * coef[0:1, cols]
                t = (p * (dpb[m128(f, FR), cols] - coef[1:2, cols])).astype(BF16)
                dv += dot(p.astype(BF16), gb[cols, :])
                dk += dot(t, qb[cols, :])
                dqt[:, cols] += dot(kt, t)
            kv[j0, m128(f, FR), 0:HEAD_WIDTH] = (scale * dk).astype(BF16)
            kv[j0, m128(f, FR), HEAD_WIDTH:2 * HEAD_WIDTH] = dv.astype(BF16)

        for d in range(1, G):
            a, _, peer, _ = gpeer(d)
            send(kv_copy(c, a, j0, peer))

    for r in range(0, NR, 128):
        dqs[pl.ds(r, 128), :] = (scale * dqt[:, pl.ds(r, 128)].T).astype(BF16)
    QR = NR // NZ

    def d_copy(z_to, z_from, peer):
        return remote(dqs.at[m128(z_to, QR)], dqin.at[z_from], ds.at[z_to], dr.at[z_from], peer)

    def a_copy(z_to, z_from, peer):
        here = dqall.at[j0, m128(z_from, QR)]
        return remote(here, here, as_.at[z_to], ar.at[z_from], peer)

    def y_copy(j_to, j_from, peer):
        here = dqall.at[j_from]
        return remote(here, here, ys.at[j_to], yr.at[j_from], peer)

    def r_copy(j, z_to, z_from, peer):
        return remote(part.at[j, m128(z_to, FB)], rsb.at[z_from, j], rs.at[j, z_to], rr.at[j, z_from], peer)

    for d in range(1, NZ):
        a, _, peer, _ = zpeer(d)
        send(d_copy(a, z, peer))
    for c in local_x:
        c.wait()
    for d in range(1, G):
        _, b, _, _ = gpeer(d)
        for i in range(NV):
            x_copy(i, j0, b, me).wait_recv()

    def weigh(j):
        @pl.loop(0, NV)
        def _(b):
            part[j, m128(b, W), :] = dot(vis[b], kv[j], TN).astype(BF16)
        for d in range(1, NZ):
            a, _, peer, _ = zpeer(d)
            send(r_copy(j, a, z, peer))

    weigh(j0)
    mine = dqs[m128(z, QR), :].astype(F32)
    for d in range(1, NZ):
        _, b, _, _ = zpeer(d)
        d_copy(z, b, me).wait_recv()
        mine += dqin[b].astype(F32)
    dqall[j0, m128(z, QR), :] = mine.astype(BF16)
    for d in range(1, NZ):
        a, _, peer, _ = zpeer(d)
        send(a_copy(a, z, peer))

    def spread():
        for d in range(1, NZ):
            _, b, _, _ = zpeer(d)
            a_copy(z, b, me).wait_recv()
        for d in range(1, G):
            a, _, peer, _ = gpeer(d)
            send(y_copy(a, j0, peer))

    if G == 1:
        spread()
    for d in range(1, G):
        _, b, _, _ = gpeer(d)
        for c in range(NC):
            kv_copy(c, j0, b, me).wait_recv()
        weigh(b)
        if d == 1:
            spread()
    for d in range(1, G):
        _, b, _, _ = gpeer(d)
        y_copy(j0, b, me).wait_recv()
    out_copy = pltpu.make_async_copy(dqall, q_out, loc.at[0])
    out_copy.start()

    for d in range(1, NZ):
        _, b, _, _ = zpeer(d)
        for j in range(G):
            r_copy(j, z, b, me).wait_recv()
    for j in range(G):
        acc = part[j, m128(z, FB), :].astype(F32)
        for d in range(1, NZ):
            _, b, _, _ = zpeer(d)
            acc += rsb[b, j].astype(F32)
        kw_out[:, pl.ds(j * HEAD_WIDTH, HEAD_WIDTH)] = acc[:, 0:HEAD_WIDTH]
        vw_out[:, pl.ds(j * HEAD_WIDTH, HEAD_WIDTH)] = acc[:, HEAD_WIDTH:]
    out_copy.wait()
    for c in sends:
        c.wait_send()


def shards(T, text_queries, text_grads, vision_keys, video_value_rows, vision, lengths, frame_range):
    R, QW = text_queries.shape
    rows, kv_width = vision_keys.shape
    G = kv_width // HEAD_WIDTH
    M = QW // kv_width
    NZ = T // G
    DW = vision.shape[1]
    blk, NK, NR = M * R, G * rows, T * M * R
    FB = DW // T
    W = FB if FB % 128 == 0 else 256
    NV = DW // (G * W)
    FR = rows // FRAME_DEV
    NC = 4 if NK >= 16 * FR else 1
    cfg = dict(T=T, G=G, NZ=NZ, blk=blk, rows=rows, NK=NK, NR=NR, FR=FR, W=W, NV=NV, FB=FB, NC=NC, RB=min(NR, 512))

    text_len = R * T
    row_ids = jnp.arange(text_len, dtype=jnp.int32)
    segment_ends = jnp.cumsum(lengths)
    segment = jnp.sum((row_ids[:, None] >= segment_ends[None, :]).astype(jnp.int32), axis=1)
    segment_pick = (
        segment[:, None] == jnp.arange(lengths.shape[0], dtype=jnp.int32)[None, :]
    ).astype(jnp.int32)
    bounds = jnp.sum(segment_pick[None] * frame_range.T[:, None, :], axis=2)
    bounds = jnp.broadcast_to(bounds.reshape(2, T, 1, R), (2, T, M, R)).reshape(2, NR)

    def split(a):
        return a.reshape(R, G, M, HEAD_WIDTH).transpose(1, 2, 0, 3).reshape(G, blk, HEAD_WIDTH)

    anyspec = pl.BlockSpec(memory_space=pl.ANY)
    vm = pl.BlockSpec(memory_space=pltpu.VMEM)
    V = pltpu.VMEM
    D = pltpu.SemaphoreType.DMA
    sem_pairs = []
    for shape in ((T,), (T,), (G,), (G,), (G, NV), (NZ,), (G, NC), (NZ,), (NZ,), (G,), (G, NZ)):
        sem_pairs += [D(shape), D(shape)]
    q_grad, kw, vw = pl.pallas_call(
        functools.partial(kernel, cfg),
        out_shape=(
            jax.ShapeDtypeStruct((G, NR, HEAD_WIDTH), BF16),
            jax.ShapeDtypeStruct((FB, kv_width), F32),
            jax.ShapeDtypeStruct((FB, kv_width), F32),
        ),
        in_specs=[anyspec] * 5 + [vm],
        out_specs=(anyspec, vm, vm),
        scratch_shapes=[
            V((NR, HEAD_WIDTH), BF16), V((NR, HEAD_WIDTH), BF16),
            V((NK, HEAD_WIDTH), BF16), V((NK, HEAD_WIDTH), BF16),
            V((NV, NK, W), BF16),
            V((NK, NR), F32), V((NK, NR), F32),
            V((8, NR), F32), V((NZ, 8, NR), F32), V((8, NR), F32),
            V((G, NK, 2 * HEAD_WIDTH), BF16),
            V((HEAD_WIDTH, NR), F32), V((NR, HEAD_WIDTH), BF16),
            V((NZ, NR // NZ, HEAD_WIDTH), BF16), V((G, NR, HEAD_WIDTH), BF16),
            V((G, DW // G, 2 * HEAD_WIDTH), BF16),
            V((NZ, G, FB, 2 * HEAD_WIDTH), BF16),
            D((4 + NV,)),
        ] + sem_pairs,
        compiler_params=pltpu.CompilerParams(
            collective_id=0, has_side_effects=True, vmem_limit_bytes=67043328
        ),
    )(split(text_queries), split(text_grads), vision_keys, video_value_rows, vision, bounds)
    q_grad = q_grad.reshape(G, T, M, R, HEAD_WIDTH).transpose(1, 3, 0, 2, 4).reshape(text_len, QW)
    return q_grad, kw, vw


def solution(mesh):
    return jax.shard_map(
        functools.partial(shards, mesh.shape["tok"]),
        mesh=mesh,
        in_specs=(
            P("tok", "head"),
            P("tok", "head"),
            P("tok", "head"),
            P("tok", "head"),
            P("tok", None),
            P(),
            P(),
        ),
        out_specs=(P(None, "head"), P("tok", "head"), P("tok", "head")),
        check_vma=False,
    )
```

time: 846 us -> 166 us (0.20); the launches traced: 832 us -> 166 us
  blocking collectives: 425 us -> 0 us
  waiting for transfers between devices: 236 us -> 0 us
  Pallas kernels: 0 us -> 153 us
  matrix products: 85.3 us -> 0 us
  local copies, waits for them, and re-layouts: 48.1 us -> 10.1 us
  other arithmetic: 17.4 us -> 1.69 us
  between operations: 13.9 us -> 0.68 us
    psum x1 -> x0, blocking collectives: 356 us -> none  [shards(): query_grad = lax.psum(query_part, 'tok').astype(jnp.bfloat16)]
    pallas_call x0 -> x1, Pallas kernels: none -> 153 us  [shards(): pl.pallas_call(functools.partial(kernel, cfg), out_shape=(jax.ShapeDtypeS...]
    all_gather x3 -> x0, waiting for transfers between devices: 129 us -> none  [the longest x1 60.5 us: shards(): lax.all_gather(text_queries, 'tok', axis=0, tiled=True)]
    psum x1 -> x0, waiting for transfers between devices: 105 us -> none  [shards(): lax.psum((local_sum * rescale, local_dot * rescale), 'tok')]
    dot_general x57 -> x0, matrix products: 85.3 us -> none  [the longest x16 25.6 us: scores_of(): jnp.einsum('ihd,jhd->hij', grad_one, value_three, preferred_element_type=...]
    pmax x1 -> x0, blocking collectives: 68.3 us -> none  [shards(): row_max = lax.pmax(local_max, 'tok')]
    unnamed x16 -> x8, local copies, waits for them, and re-layouts: 23.2 us -> 3.44 us
  transfers between devices with their start and end apart: 5 -> 0, of which waited for: 4 -> 0; matrix products, arithmetic and copies ran while one was open for 4% -> 0% of each run, Pallas kernels for 0% -> 0%
where the time goes in v1:
time: 166 us
  Pallas kernels  153 us (92%)
  local copies, waits for them, and re-layouts  10.1 us (6%)
  other arithmetic  1.69 us (1%)
    pallas_call x1, Pallas kernels, shards(): pl.pallas_call(functools.partial(kernel, cfg), out_shape=(jax.ShapeDtypeS...  153 us
    unnamed x8, local copies, waits for them, and re-layouts  3.44 us

profile of v1, /device:TPU:8, one launch (start us, length us, event | category | flops | bytes accessed | tf_op | source)
XLA Modules:
  0.0 165.9 jit_solution(3336543067285148696)
XLA Ops:
  0.6 0.8 reduce-window.8
  1.5 0.1 convert_reduce_fusion
  1.6 0.8 multiply_reduce_fusion
  2.3 0.1 broadcast_in_dim.4
  2.4 0.7 reshape.79.bounds
  3.1 0.9 copy.16
  4.1 0.7 copy.13
  4.8 0.9 copy.17
  5.7 0.7 copy.14
  6.4 153.5 %shard_map.94 = (bf16[4,2048,128]{2,1,0:T(8,128)(2,1)}, f32[256,512]{1,0:T(8,128)}, f32[256,512]{1,0:T(8,128)}) custom-call(bf16[4,128,128]{2,1,0:T(8,128)(2,1)} %bitcast.23, bf16[4,128,128]{2,1,0:T(8,128)(2,1)} %bitcast.24, bf16[512,512]{1,0:T(8,128)(2,1)} %k_in.1, bf16[512,512]{1,0:T(8,128)(2,1)} %v_in.1, bf16[512,4096]{1,0:T(8,128)(2,1)} %x_in.1, ...), custom_call_target="tpu_custom_call" | custom-call | tf_op jit(solution)/shard_map/pallas_call | solution.py:307
  159.9 2.1 %copy.15 = bf16[16,16,4,8,128]{4,3,2,1,0:T(8,128)(2,1)S(1)} copy(bf16[16,16,4,8,128]{4,1,3,0,2:T(8,128)(2,1)} %bitcast.22) | data formatting | bytes 4194304 | tf_op jit(solution)/shard_map/transpose | solution.py:333
  162.0 0.0 copy-start.1
  162.0 0.0 copy-start
  162.0 2.3 %reshape.81 = bf16[256,4096]{1,0:T(8,128)(2,1)} reshape(bf16[16,16,4,8,128]{4,3,2,1,0:T(8,128)(2,1)S(1)} %copy.15) | data formatting | bytes 4194304 | tf_op jit(solution)/shard_map/reshape | solution.py:333
  164.3 0.0 copy-done.1
  164.3 0.8 copy.20
  165.1 0.0 copy-done
  165.1 0.8 copy.21
  (2 shorter events, 0.0 us)
Async XLA Ops:
  162.0 2.3 %copy-start.1 = (f32[256,512]{1,0:T(8,128)S(1)}, f32[256,512]{1,0:T(8,128)}, u32[]{:S(2)}) copy-start(f32[256,512]{1,0:T(8,128)} %get-tuple-element.13) | copy-start | bytes 1572868
  162.0 3.1 %copy-start = (f32[256,512]{1,0:T(8,128)S(1)}, f32[256,512]{1,0:T(8,128)}, u32[]{:S(2)}) copy-start(f32[256,512]{1,0:T(8,128)} %get-tuple-element.14) | copy-start | bytes 1572868

commit v2 on v1

--- a/solution.py
+++ b/solution.py
@@ -22,10 +22,11 @@
 
 def kernel(cfg, q_in, g_in, k_in, v_in, x_in, bounds, q_out, kw_out, vw_out,
            qb, gb, kb, vb, vis, ebuf, dpb, stat, stin, coef, kv, dqt, dqs, dqin, dqall, part, rsb,
-           loc, qs, qr, gs, gr, ks, kr, vs, vr, xs, xr, ss, sr, kvs, kvr, ds, dr, as_, ar, ys, yr, rs, rr):
+           loc, qs, qr, gs, gr, ks, kr, vs, vr, xs, xr, ss, sr, kvs, kvr, ds, dr, as_, ar, ys, yr, rs, rr, fs, fr):
     T, G, NZ = cfg["T"], cfg["G"], cfg["NZ"]
     blk, rows, NK, NR, FR = cfg["blk"], cfg["rows"], cfg["NK"], cfg["NR"], cfg["FR"]
     W, NV, FB = cfg["W"], cfg["NV"], cfg["FB"]
+    H = cfg["H"]
     RB = cfg["RB"]
     scale = HEAD_WIDTH ** (-0.5)
     me = lax.axis_index("tok")
@@ -42,13 +43,17 @@
     barrier = pltpu.get_barrier_semaphore()
     for d in range(1, T):
         pl.semaphore_signal(barrier, inc=1, device_id={"tok": lax.rem(me + d, T)}, device_id_type=pl.DeviceIdType.MESH)
-    pl.semaphore_wait(barrier, T - 1)
+    twin = lax.axis_index("head")
+    if H > 1:
+        twin = 1 - twin
+        pl.semaphore_signal(barrier, inc=1, device_id={"head": twin}, device_id_type=pl.DeviceIdType.MESH)
+    pl.semaphore_wait(barrier, T - 1 + (H > 1))
 
     def tpeer(d):
         return lax.rem(me + d, T), lax.rem(me + T - d, T)
 
     def gpeer(d):
-        a, b = lax.rem(j0 + d, G), lax.rem(j0 + G - d, G)
+        a, b = (j0 ^ d, j0 ^ d) if G & (G - 1) == 0 else (lax.rem(j0 + d, G), lax.rem(j0 + G - d, G))
         return a, b, z * G + a, z * G + b
 
     def zpeer(d):
@@ -69,8 +74,20 @@
         return (remote(k_in.at[:, m128(j_to, 128)], kb.at[m128(j_from, rows)], ks.at[j_to], kr.at[j_from], peer),
                 remote(v_in.at[:, m128(j_to, 128)], vb.at[m128(j_from, rows)], vs.at[j_to], vr.at[j_from], peer))
 
+    WH = W // H
+    half = lax.axis_index("head") * WH if H > 1 else 0
+
     def x_copy(b, j_to, j_from, peer):
-        return remote(x_in.at[:, m128(b * G + j_to, W)], vis.at[b, m128(j_from, rows)], xs.at[j_to, b], xr.at[j_from, b], peer)
+        cols = pl.ds(pl.multiple_of((b * G + j_to) * W + half, WH), WH)
+        dst = vis.at[b, m128(j_from, rows), pl.ds(pl.multiple_of(half, WH), WH)]
+        return remote(x_in.at[:, cols], dst, xs.at[j_to, b], xr.at[j_from, b], peer)
+
+    def f_copy(b, j_from, mine):
+        at = half if mine else WH - half
+        here = vis.at[b, m128(j_from, rows), pl.ds(pl.multiple_of(at, WH), WH)]
+        return pltpu.make_async_remote_copy(
+            src_ref=here, dst_ref=here, send_sem=fs.at[j_from, b], recv_sem=fr.at[j_from, b],
+            device_id={"head": twin}, device_id_type=pl.DeviceIdType.MESH)
 
     local = [
         pltpu.make_async_copy(q_in.at[j0], qb.at[m128(me, blk)], loc.at[0]),
@@ -81,57 +98,92 @@
     local_x = [pltpu.make_async_copy(x_in.at[:, m128(b * G + j0, W)], vis.at[b, m128(j0, rows)], loc.at[4 + b]) for b in range(NV)]
     for c in local:
         c.start()
-    for d in range(1, T):
-        to, _ = tpeer(d)
-        for c in q_copy(to, me):
-            send(c)
+    def q_sends(zd):
+        a, _, _, _ = zpeer(zd)
+        for i in range(G):
+            to = a * G + (lax.rem(j0 + i, G) if zd else gpeer(i)[0])
+            if zd or i:
+                for c in q_copy(to, me):
+                    send(c)
+
+    q_sends(0)
     for d in range(1, G):
         a, _, peer, _ = gpeer(d)
         for c in k_copy(a, j0, peer):
             send(c)
+    for d in range(1, NZ):
+        q_sends(d)
     for c in local_x:
         c.start()
-    for d in range(1, G):
-        a, _, peer, _ = gpeer(d)
-        for b in range(NV):
-            send(x_copy(b, a, j0, peer))
     for c in local:
         c.wait()
     for d in range(1, G):
         _, b, _, _ = gpeer(d)
         for c in k_copy(j0, b, me):
             c.wait_recv()
-    for d in range(1, T):
-        _, frm = tpeer(d)
-        for c in q_copy(me, frm):
-            c.wait_recv()
+
+    def q_wait(zd):
+        _, b, _, _ = zpeer(zd)
+        for i in range(G):
+            if zd or i:
+                frm = b * G + (i if zd else gpeer(i)[1])
+                for c in q_copy(me, frm):
+                    c.wait_recv()
 
     n_frames = NK // FR
     frame0 = z * n_frames
     stat[0:1, :] = jnp.full((1, NR), NEG_FILL, F32)
     stat[1:8, :] = jnp.zeros((7, NR), F32)
 
-    @pl.loop(0, n_frames)
-    def _(f):
-        kc = kb[m128(f, FR), :]
+    def totals(cols, width):
+        first, end = bounds[0:1, cols], bounds[1:2, cols]
+        UN = 2 if n_frames % 2 == 0 else 1
+
+        def scored(i, top):
+            for u in range(UN):
+                f = i * UN + u
+                ok = (first <= frame0 + f) & (frame0 + f < end)
+                s = jnp.where(ok, dot(kb[m128(f, FR), :], qb[cols, :], NT) * scale, NEG_FILL)
+                ebuf[m128(f, FR), cols] = s
+                top = jnp.maximum(top, jnp.max(s, axis=0, keepdims=True))
+            return top
+
+        top = lax.fori_loop(0, n_frames // UN, scored, jnp.full((1, width), NEG_FILL, F32))
+
+        def summed(i, carry):
+            total, dotted = carry
+            for u in range(UN):
+                f = i * UN + u
+                dp = dot(vb[m128(f, FR), :], gb[cols, :], NT)
+                e = jnp.exp(ebuf[m128(f, FR), cols] - top)
+                ebuf[m128(f, FR), cols] = e
+                dpb[m128(f, FR), cols] = dp
+                total += jnp.sum(e, axis=0, keepdims=True)
+                dotted += jnp.sum(e * dp, axis=0, keepdims=True)
+            return total, dotted
+
+        zero = jnp.zeros((1, width), F32)
+        total, dotted = lax.fori_loop(0, n_frames // UN, summed, (zero, zero))
+        stat[0:1, cols] = top
+        stat[1:2, cols] = total
+        stat[2:3, cols] = dotted
+
+    def x_sends():
+        for d in range(1, G):
+            a, _, peer, _ = gpeer(d)
+            for b in range(NV):
+                send(x_copy(b, a, j0, peer))
+
+    by_z = (NR // NZ) % 128 == 0
+    for d in range(NZ):
+        q_wait(d)
+        if d == NZ - 1:
+            x_sends()
+        if by_z:
+            totals(m128(zpeer(d)[1], NR // NZ), NR // NZ)
+    if not by_z:
         for r in range(0, NR, RB):
-            cols = pl.ds(r, RB)
-            ok = (bounds[0:1, cols] <= frame0 + f) & (frame0 + f < bounds[1:2, cols])
-            s = jnp.where(ok, dot(kc, qb[cols, :], NT) * scale, NEG_FILL)
-            ebuf[m128(f, FR), cols] = s
-            stat[0:1, cols] = jnp.maximum(stat[0:1, cols], jnp.max(s, axis=0, keepdims=True))
-
-    @pl.loop(0, n_frames)
-    def _(f):
-        vc = vb[m128(f, FR), :]
-        for r in range(0, NR, RB):
-            cols = pl.ds(r, RB)
-            dp = dot(vc, gb[cols, :], NT)
-            e = jnp.exp(ebuf[m128(f, FR), cols] - stat[0:1, cols])
-            ebuf[m128(f, FR), cols] = e
-            dpb[m128(f, FR), cols] = dp
-            stat[1:2, cols] += jnp.sum(e, axis=0, keepdims=True)
-            stat[2:3, cols] += jnp.sum(e * dp, axis=0, keepdims=True)
+            totals(pl.ds(r, RB), RB)
 
     def s_copy(z_to, z_from, peer):
         return remote(stat, stin.at[z_from], ss.at[z_to], sr.at[z_from], peer)
@@ -179,9 +231,15 @@
             kv[j0, m128(f, FR), 0:HEAD_WIDTH] = (scale * dk).astype(BF16)
             kv[j0, m128(f, FR), HEAD_WIDTH:2 * HEAD_WIDTH] = dv.astype(BF16)
 
-        for d in range(1, G):
+        for d in range(1, G - 1):
             a, _, peer, _ = gpeer(d)
-            send(kv_copy(c, a, j0, peer))
+            kv_copy(c, a, j0, peer).start()
+        if H > 1 and c == NC // 2:
+            for d in range(1, G):
+                _, b, _, _ = gpeer(d)
+                for i in range(NV):
+                    x_copy(i, j0, b, me).wait_recv()
+                    send(f_copy(i, b, True))
 
     for r in range(0, NR, 128):
         dqs[pl.ds(r, 128), :] = (scale * dqt[:, pl.ds(r, 128)].T).astype(BF16)
@@ -209,7 +267,7 @@
     for d in range(1, G):
         _, b, _, _ = gpeer(d)
         for i in range(NV):
-            x_copy(i, j0, b, me).wait_recv()
+            (f_copy(i, b, False) if H > 1 else x_copy(i, j0, b, me)).wait_recv()
 
     def weigh(j):
         @pl.loop(0, NV)
@@ -238,6 +296,14 @@
             a, _, peer, _ = gpeer(d)
             send(y_copy(a, j0, peer))
 
+    for d in range(1, G - 1):
+        a, _, peer, _ = gpeer(d)
+        for c in range(NC):
+            kv_copy(c, a, j0, peer).wait_send()
+    if G > 1:
+        a, _, peer, _ = gpeer(G - 1)
+        for c in range(NC):
+            send(kv_copy(c, a, j0, peer))
     if G == 1:
         spread()
     for d in range(1, G):
@@ -245,7 +311,7 @@
         for c in range(NC):
             kv_copy(c, j0, b, me).wait_recv()
         weigh(b)
-        if d == 1:
+        if d == min(2, G - 1):
             spread()
     for d in range(1, G):
         _, b, _, _ = gpeer(d)
@@ -269,7 +335,7 @@
         c.wait_send()
 
 
-def shards(T, text_queries, text_grads, vision_keys, video_value_rows, vision, lengths, frame_range):
+def shards(T, cores, text_queries, text_grads, vision_keys, video_value_rows, vision, lengths, frame_range):
     R, QW = text_queries.shape
     rows, kv_width = vision_keys.shape
     G = kv_width // HEAD_WIDTH
@@ -282,7 +348,8 @@
     NV = DW // (G * W)
     FR = rows // FRAME_DEV
     NC = 4 if NK >= 16 * FR else 1
-    cfg = dict(T=T, G=G, NZ=NZ, blk=blk, rows=rows, NK=NK, NR=NR, FR=FR, W=W, NV=NV, FB=FB, NC=NC, RB=min(NR, 512))
+    cfg = dict(T=T, G=G, NZ=NZ, blk=blk, rows=rows, NK=NK, NR=NR, FR=FR, W=W, NV=NV, FB=FB, NC=NC, RB=min(NR, 512),
+               H=2 if cores == 2 and G > 1 and W % 256 == 0 else 1)
 
     text_len = R * T
     row_ids = jnp.arange(text_len, dtype=jnp.int32)
@@ -302,7 +369,7 @@
     V = pltpu.VMEM
     D = pltpu.SemaphoreType.DMA
     sem_pairs = []
-    for shape in ((T,), (T,), (G,), (G,), (G, NV), (NZ,), (G, NC), (NZ,), (NZ,), (G,), (G, NZ)):
+    for shape in ((T,), (T,), (G,), (G,), (G, NV), (NZ,), (G, NC), (NZ,), (NZ,), (G,), (G, NZ), (G, NV)):
         sem_pairs += [D(shape), D(shape)]
     q_grad, kw, vw = pl.pallas_call(
         functools.partial(kernel, cfg),
@@ -336,7 +403,7 @@
 
 def solution(mesh):
     return jax.shard_map(
-        functools.partial(shards, mesh.shape["tok"]),
+        functools.partial(shards, mesh.shape["tok"], mesh.shape["head"]),
         mesh=mesh,
         in_specs=(
             P("tok", "head"),

time: 166 us -> 154 us (0.928)
  Pallas kernels: 153 us -> 142 us
    pallas_call x1, Pallas kernels: 153 us -> 142 us  [shards(): pl.pallas_call(functools.partial(kernel, cfg), out_shape=(jax.ShapeDtypeS...]
where the time goes in v2:
time: 154 us
  Pallas kernels  142 us (92%)
  local copies, waits for them, and re-layouts  10.1 us (7%)
  other arithmetic  1.69 us (1%)
    pallas_call x1, Pallas kernels, shards(): pl.pallas_call(functools.partial(kernel, cfg), out_shape=(jax.ShapeDtypeS...  142 us
    unnamed x8, local copies, waits for them, and re-layouts  3.44 us

profile of v2, /device:TPU:8, one launch (start us, length us, event | category | flops | bytes accessed | tf_op | source)
XLA Modules:
  0.0 154.2 jit_solution(12704774017387122721)
XLA Ops:
  0.6 0.8 reduce-window.8
  1.5 0.1 convert_reduce_fusion
  1.6 0.8 multiply_reduce_fusion
  2.3 0.1 broadcast_in_dim.4
  2.4 0.7 reshape.79.bounds
  3.1 0.9 copy.16
  4.1 0.7 copy.13
  4.8 0.9 copy.17
  5.7 0.7 copy.14
  6.4 141.7 %shard_map.94 = (bf16[4,2048,128]{2,1,0:T(8,128)(2,1)}, f32[256,512]{1,0:T(8,128)}, f32[256,512]{1,0:T(8,128)}) custom-call(bf16[4,128,128]{2,1,0:T(8,128)(2,1)} %bitcast.23, bf16[4,128,128]{2,1,0:T(8,128)(2,1)} %bitcast.24, bf16[512,512]{1,0:T(8,128)(2,1)} %k_in.1, bf16[512,512]{1,0:T(8,128)(2,1)} %v_in.1, bf16[512,4096]{1,0:T(8,128)(2,1)} %x_in.1, ...), custom_call_target="tpu_custom_call" | custom-call | tf_op jit(solution)/shard_map/pallas_call | solution.py:374
  148.1 2.1 %copy.15 = bf16[16,16,4,8,128]{4,3,2,1,0:T(8,128)(2,1)S(1)} copy(bf16[16,16,4,8,128]{4,1,3,0,2:T(8,128)(2,1)} %bitcast.22) | data formatting | bytes 4194304 | tf_op jit(solution)/shard_map/transpose | solution.py:400
  150.3 0.0 copy-start.1
  150.3 0.0 copy-start
  150.3 2.3 %reshape.81 = bf16[256,4096]{1,0:T(8,128)(2,1)} reshape(bf16[16,16,4,8,128]{4,3,2,1,0:T(8,128)(2,1)S(1)} %copy.15) | data formatting | bytes 4194304 | tf_op jit(solution)/shard_map/reshape | solution.py:400
  152.6 0.0 copy-done.1
  152.6 0.8 copy.20
  153.4 0.0 copy-done
  153.4 0.8 copy.21
  (2 shorter events, 0.0 us)
Async XLA Ops:
  150.3 2.3 %copy-start.1 = (f32[256,512]{1,0:T(8,128)S(1)}, f32[256,512]{1,0:T(8,128)}, u32[]{:S(2)}) copy-start(f32[256,512]{1,0:T(8,128)} %get-tuple-element.13) | copy-start | bytes 1572868
  150.3 3.1 %copy-start = (f32[256,512]{1,0:T(8,128)S(1)}, f32[256,512]{1,0:T(8,128)}, u32[]{:S(2)}) copy-start(f32[256,512]{1,0:T(8,128)} %get-tuple-element.14) | copy-start | bytes 1572868
